TPU v7x, 32 devices: a whole 2x2x4 slice. The times are simulated.
32 devices in a mesh: dp: 2 (over x), crop: 4 (over y, core), tensor: 4 (over z).
Axes of the slice: x: 2, y: 2, z: 4, core: 2. Of those that a mesh axis runs over, the one named last changes fastest.
Arguments:
- hidden_a: bfloat16 [512, 8192], P('crop', 'dp'), as said below
- hidden_b: bfloat16 [512, 8192], P('crop', 'dp'), as said below
- weight: bfloat16 [8192, 8192], P('dp', 'tensor')
Outputs:
- weight_grad: float32 [8192, 8192], P(('dp', 'crop'), 'tensor')
Inputs may be any that keep to these rules, and one draw needn't show every extreme that they name: `hidden_a`: nonnegative entries. `hidden_b`: nonnegative entries.
All inputs are finite; a program needn't handle non-finite values.
Results may differ from a plain program's by a relative error of at most 0.0015.
Values may be sent and summed in bfloat16 or wider, within the bound.
A program may use at most 128 MiB of HBM per device.

v0:
```python
import jax
import jax.numpy as jnp
from jax import lax
from jax.sharding import PartitionSpec as P

epsilon = 0.0001


def body(hidden_a, hidden_b, weight):
    group_size = lax.axis_size(("dp", "crop"))
    data_count = lax.axis_size("dp")
    block_rows = hidden_a.shape[0]
    local_rows = block_rows // data_count
    total_rows = local_rows * group_size
    left_part = jnp.dot(hidden_a, weight, preferred_element_type=jnp.float32)
    right_part = jnp.dot(hidden_b, weight, preferred_element_type=jnp.float32)
    joined = lax.psum_scatter(
        jnp.stack([left_part, right_part], axis=1), "dp", scatter_dimension=0, tiled=True
    ).astype(jnp.bfloat16)
    stacked = jnp.stack([joined[:, 0, :], joined[:, 1, :]]).astype(jnp.float32)
    col_means = lax.psum(jnp.sum(stacked, axis=1), ("dp", "crop")) / total_rows
    centered = stacked - col_means[:, None, :]
    spread = lax.psum(jnp.sum(centered * centered, axis=1), ("dp", "crop"))
    deviation = jnp.sqrt(spread / (total_rows - 1.0) + epsilon)
    rounded = centered.astype(jnp.bfloat16)
    everyone = lax.all_gather(rounded, ("dp", "crop"), axis=1, tiled=True)
    gram = jnp.einsum("vrf,vbf->vrb", rounded, everyone, preferred_element_type=jnp.float32)
    gram = lax.psum(gram, "tensor")
    gram_low = gram.astype(jnp.bfloat16)
    products = jnp.einsum("vrb,vbf->vrf", gram_low, everyone, preferred_element_type=jnp.float32)
    hinge_rate = jnp.where(deviation < 1.0, 25.0 / ((total_rows - 1.0) * deviation), 0.0)[
        :, None, :
    ]
    differ = stacked[0] - stacked[1]
    pull_term = jnp.stack([differ, -differ]) * (50.0 / total_rows)
    cov_scale = 4.0 / (total_rows - 1.0) ** 2
    row_grads = (
        pull_term - hinge_rate * centered + cov_scale * (products - centered * spread[:, None, :])
    )
    row_grads = row_grads.astype(jnp.bfloat16)
    block_grads = lax.all_gather(row_grads, "dp", axis=1, tiled=True)
    across = (((0,), (0,)), ((), ()))
    left_part = lax.dot_general(
        hidden_a, block_grads[0], across, preferred_element_type=jnp.float32
    )
    right_part = lax.dot_general(
        hidden_b, block_grads[1], across, preferred_element_type=jnp.float32
    )
    return lax.psum_scatter(left_part + right_part, "crop", scatter_dimension=0, tiled=True)


def solution(mesh):
    placed = (P("crop", "dp"), P("crop", "dp"), P("dp", "tensor"))
    return jax.shard_map(
        body, mesh=mesh, in_specs=placed, out_specs=P(("dp", "crop"), "tensor"), check_vma=False
    )
```

profile of v0, /device:TPU:0, one launch (start us, length us, event | category | flops | bytes accessed | tf_op | source)
XLA Modules:
  0.0 458.1 jit_solution(6418926525455714938)
XLA Ops:
  6.5 1.2 copy-done
  7.8 8.2 %convolution_bitcast_fusion.1 = f32[128,1,2048]{2,0,1:T(8,128)S(1)} fusion(bf16[128,4096]{1,0:T(8,128)(2,1)S(1)} %copy-done, bf16[4096,2048]{1,0:T(8,128)(2,1)} %param.5), kind=kOutput, calls=%fused_computation.5 | convolution fusion | flops 2147483648 | bytes 18874368 | tf_op jit(solution)/shard_map/dot_general | solution.py:15
  16.0 2.4 copy-done.2
  18.4 2.4 convolution_bitcast_fusion
  20.8 1.5 pad_maximum_fusion
  22.3 34.7 %reduce-scatter.3.cloned.1.call-done = f32[64,2,2048]{2,0,1:T(8,128)} async-done(((f32[128,2,2048]{2,0,1:T(8,128)}), f32[64,2,2048]{2,0,1:T(8,128)}) %reduce-scatter.3.cloned.1.call-update) | async-done | bytes 1048592 | tf_op jit(solution)/shard_map/reduce_scatter | solution.py:17
  57.1 1.3 convert_element_type.15
  58.4 0.1 convert_reduce_fusion
  58.5 22.9 %psum.21 = f32[2,2048]{1,0:T(2,128)S(1)} all-reduce(f32[2,2048]{1,0:T(2,128)S(1)} %convert_reduce_fusion), channel_id=1, replica_groups=mesh['dp'=2,'crop'=4,'tensor'=4] {'dp','crop'}, use_global_device_ids=true, to_apply=%region_2.0 | all-reduce | flops 4096 | bytes 32768 | tf_op jit(solution)/shard_map/psum | solution.py:21
  81.5 1.0 multiply_reduce_fusion
  82.5 22.7 %psum.22 = f32[2,2048]{1,0:T(2,128)S(1)} all-reduce(f32[2,2048]{1,0:T(2,128)S(1)} %get-tuple-element.7), channel_id=1, replica_groups=mesh['dp'=2,'crop'=4,'tensor'=4] {'dp','crop'}, use_global_device_ids=true, to_apply=%region_4.0 | all-reduce | flops 4096 | bytes 32768 | tf_op jit(solution)/shard_map/psum | solution.py:23
  105.3 0.5 copy-done.5
  105.8 0.6 compare_select_fusion
  106.4 0.9 fusion.7
  107.3 12.0 %all-gather.3.cloned.1.call-done = bf16[2,512,2048]{2,1,0:T(8,128)(2,1)} async-done(((bf16[2,64,2048]{2,1,0:T(8,128)(2,1)}), bf16[2,512,2048]{2,1,0:T(8,128)(2,1)}) %all-gather.3.cloned.1.call-update) | async-done | bytes 4194320 | tf_op jit(solution)/shard_map/all_gather | solution.py:26
  119.3 3.7 fusion.8
  123.1 24.7 %all-reduce.1 = bf16[2,64,512]{2,1,0:T(8,128)(2,1)S(1)} all-reduce(f32[2,64,512]{2,1,0:T(8,128)S(1)} %fusion.8), channel_id=1, replica_groups=mesh['dp'=2,'crop'=4,'tensor'=4] {'tensor'}, use_global_device_ids=true, to_apply=%region_5.0 | all-reduce | flops 65536 | bytes 393216 | tf_op jit(solution)/shard_map/psum | solution.py:28
  147.7 4.2 fusion.2
  152.0 0.2 reduce-scatter.5.cloned.1.call-start
  152.2 18.8 %all-gather.5.cloned.1.call-done = bf16[2,128,2048]{2,1,0:T(8,128)(2,1)} async-done(((bf16[2,64,2048]{2,1,0:T(8,128)(2,1)}), bf16[2,128,2048]{2,1,0:T(8,128)(2,1)}) %all-gather.5.cloned.1.call-update) | async-done | bytes 1048592 | tf_op jit(solution)/shard_map/all_gather | solution.py:41
  171.0 14.3 %fusion.4 = f32[2048,4096]{1,0:T(8,128)} fusion(bf16[128,4096]{1,0:T(8,128)(2,1)S(1)} %copy-done, bf16[2,128,2048]{2,1,0:T(8,128)(2,1)} %all-gather.5.cloned.1.call-done), kind=kOutput, calls=%fused_computation.15 | convolution fusion | flops 2147483648 | bytes 35127296 | tf_op jit(solution)/shard_map/dot_general | solution.py:43
  185.3 24.8 %add_bitcast_fusion = f32[4096,2048]{0,1:T(8,128)} fusion(f32[2048,4096]{1,0:T(8,128)} %fusion.4, bf16[128,4096]{1,0:T(8,128)(2,1)S(1)} %copy-done.3, bf16[2,128,2048]{2,1,0:T(8,128)(2,1)S(1)} %copy-done.4), kind=kOutput, calls=%fused_computation | convolution fusion | flops 2155872256 | bytes 68681728 | tf_op jit(solution)/shard_map/dot_general | solution.py:46
  210.1 232.3 %reduce-scatter.5.cloned.1.call-done = f32[1024,2048]{0,1:T(8,128)} async-done(((f32[4096,2048]{0,1:T(8,128)}), f32[1024,2048]{0,1:T(8,128)}) %reduce-scatter.5.cloned.1.call-update) | async-done | bytes 8388624 | tf_op jit(solution)/shard_map/reduce_scatter | solution.py:49
  442.4 9.1 %copy.4 = f32[1024,2048]{1,0:T(8,128)} copy(f32[1024,2048]{0,1:T(8,128)} %reduce-scatter.5.cloned.1.call-done) | data formatting | bytes 16777216 | tf_op jit(solution)/shard_map/reduce_scatter | solution.py:49
  (19 shorter events, 0.3 us)
Async XLA Ops:
  6.5 1.2 copy-start
  6.5 9.5 %copy-start.3 = (bf16[128,4096]{1,0:T(8,128)(2,1)S(1)}, bf16[128,4096]{1,0:T(8,128)(2,1)}, u32[]{:S(2)}) copy-start(bf16[128,4096]{1,0:T(8,128)(2,1)} %param.4) | copy-start | bytes 3145732
  6.5 50.5 %reduce-scatter.3.cloned.1.call-start = ((), (), s32[]{:S(2)}) async-start(), calls=%async_computation.2 | async-start | bytes 3145728 | tf_op jit(solution)/shard_map/reduce_scatter | solution.py:17
  7.8 10.6 %copy-start.2 = (bf16[4096,2048]{1,0:T(8,128)(2,1)S(1)}, bf16[4096,2048]{1,0:T(8,128)(2,1)}, u32[]{:S(2)}) copy-start(bf16[4096,2048]{1,0:T(8,128)(2,1)} %param.5) | copy-start | bytes 50331652
  22.3 97.0 %all-gather.3.cloned.1.call-start = ((), (), s32[]{:S(2)}) async-start(), calls=%async_computation.3 | async-start | bytes 4718592 | tf_op jit(solution)/shard_map/all_gather | solution.py:26
  82.4 88.5 %all-gather.5.cloned.1.call-start = ((), (), s32[]{:S(2)}) async-start(), calls=%async_computation.4 | async-start | bytes 1572864 | tf_op jit(solution)/shard_map/all_gather | solution.py:41
  105.2 0.6 copy-start.5
  152.0 290.4 %reduce-scatter.5.cloned.1.call-start = ((), (), s32[]{:S(2)}) async-start(), calls=%async_computation.5 | async-start | bytes 41943040 | tf_op jit(solution)/shard_map/reduce_scatter | solution.py:49
  171.0 14.3 %copy-start.4 = (bf16[2,128,2048]{2,1,0:T(8,128)(2,1)S(1)}, bf16[2,128,2048]{2,1,0:T(8,128)(2,1)}, u32[]{:S(2)}) copy-start(bf16[2,128,2048]{2,1,0:T(8,128)(2,1)} %all-gather.5.cloned.1.call-done) | copy-start | bytes 3145732
  210.1 241.5 %copy-start.1 = (bf16[128,4096]{1,0:T(8,128)(2,1)S(1)}, bf16[128,4096]{1,0:T(8,128)(2,1)}, u32[]{:S(2)}) copy-start(bf16[128,4096]{1,0:T(8,128)(2,1)} %param.3) | copy-start | bytes 3145732
Sparse Core Ops, SparseCore 0:
  22.4 34.6 reduce-scatter.2
  82.6 36.6 all-gather.2
  152.1 18.8 all-gather.4
  210.2 232.1 reduce-scatter.4
where the time goes:
time: 458 us
  waiting for transfers between devices  298 us (65%)
  blocking collectives  70.3 us (15%)
  matrix products  57.7 us (13%)
  local copies, waits for them, and re-layouts  13.3 us (3%)
  between operations  13.2 us (3%)
  other arithmetic  5.43 us (1%)
    reduce_scatter x1, waiting for transfers between devices, body(): lax.psum_scatter(left_part + right_part, 'crop', scatter_dimension=0, til...  232 us
    reduce_scatter x1, waiting for transfers between devices, body(): lax.psum_scatter(jnp.stack([left_part, right_part], axis=1), 'dp', scatte...  34.7 us
    dot_general x1, matrix products, body(): lax.dot_general(hidden_b, block_grads[1], across, preferred_element_type=...  24.8 us
    psum x1, blocking collectives, body(): gram = lax.psum(gram, 'tensor')  24.7 us
    psum x1, blocking collectives, body(): col_means = lax.psum(jnp.sum(stacked, axis=1), ('dp', 'crop')) / total_rows  22.9 us
    psum x1, blocking collectives, body(): spread = lax.psum(jnp.sum(centered * centered, axis=1), ('dp', 'crop'))  22.7 us
    all_gather x1, waiting for transfers between devices, body(): block_grads = lax.all_gather(row_grads, 'dp', axis=1, tiled=True)  18.8 us
    dot_general x1, matrix products, body(): lax.dot_general(hidden_a, block_grads[0], across, preferred_element_type=...  14.3 us
  transfers between devices with their start and end apart: 4, of which 4 were waited for; matrix products, arithmetic and copies ran while one was open for 0% of the time, Pallas kernels for 0%

commit v1 on v0

v1 whole, which is shorter than its diff:
```python
import jax
import jax.numpy as jnp
from jax import lax
from jax.sharding import PartitionSpec as P

epsilon = 0.0001
f32 = jnp.float32
bf16 = jnp.bfloat16


def gather_features(hidden, weight):
    left = jnp.dot(hidden[0], weight, preferred_element_type=f32)
    right = jnp.dot(hidden[1], weight, preferred_element_type=f32)
    mine = lax.psum_scatter(
        jnp.stack([left, right], axis=1), "dp", scatter_dimension=0, tiled=True
    ).astype(bf16)
    whole = lax.all_gather(mine, ("crop", "dp"), axis=0, tiled=True)
    return jnp.stack([whole[:, 0, :], whole[:, 1, :]])


def share_gram(rounded):
    groups = lax.axis_size("dp") * lax.axis_size("crop")
    rows = rounded.shape[1] // groups
    place = lax.axis_index("crop") * lax.axis_size("dp") + lax.axis_index("dp")
    own = lax.dynamic_slice_in_dim(rounded, place * rows, rows, axis=1)
    gram = jnp.einsum("vrf,vbf->vrb", own, rounded, preferred_element_type=f32)
    gram = lax.psum(gram, "tensor").astype(bf16)
    return lax.all_gather(gram, ("crop", "dp"), axis=1, tiled=True)


def body(hidden_a, hidden_b, weight):
    hidden = jnp.stack([hidden_a, hidden_b])
    columns = lax.all_to_all(hidden, "crop", split_axis=2, concat_axis=1, tiled=True)
    low = gather_features((hidden_a, hidden_b), weight)
    stacked = low.astype(f32)
    total_rows = stacked.shape[1]
    col_means = jnp.mean(stacked, axis=1)
    centered = stacked - col_means[:, None, :]
    spread = jnp.sum(centered * centered, axis=1)
    deviation = jnp.sqrt(spread / (total_rows - 1.0) + epsilon)
    rounded = centered.astype(bf16)
    gram_low = share_gram(rounded)
    products = jnp.einsum("vrb,vbf->vrf", gram_low, rounded, preferred_element_type=f32)
    hinge_rate = jnp.where(deviation < 1.0, 25.0 / ((total_rows - 1.0) * deviation), 0.0)[
        :, None, :
    ]
    differ = stacked[0] - stacked[1]
    pull_term = jnp.stack([differ, -differ]) * (50.0 / total_rows)
    cov_scale = 4.0 / (total_rows - 1.0) ** 2
    row_grads = (
        pull_term - hinge_rate * centered + cov_scale * (products - centered * spread[:, None, :])
    ).astype(bf16)
    both = columns.reshape(2 * total_rows, -1)
    grads = row_grads.reshape(2 * total_rows, -1)
    across = (((0,), (0,)), ((), ()))
    return lax.dot_general(both, grads, across, preferred_element_type=f32)


def solution(mesh):
    placed = (P("crop", "dp"), P("crop", "dp"), P("dp", "tensor"))
    return jax.shard_map(
        body, mesh=mesh, in_specs=placed, out_specs=P(("dp", "crop"), "tensor"), check_vma=False
    )
```

time: 458 us -> 184 us (0.40)
  waiting for transfers between devices: 298 us -> 84.1 us
  blocking collectives: 70.3 us -> 25.3 us
  matrix products: 57.7 us -> 26.4 us
  other arithmetic: 5.43 us -> 13.6 us
    reduce_scatter x2 -> x1, waiting for transfers between devices: 267 us -> 34.7 us  [gather_features(): lax.psum_scatter(jnp.stack([left, right], axis=1), 'dp', scatter_dimensio...]
    psum x3 -> x1, blocking collectives: 70.3 us -> 25.3 us  [share_gram(): gram = lax.psum(gram, 'tensor').astype(bf16)]
    dot_general x6 -> x5, matrix products: 57.7 us -> 26.4 us  [the longest x1 8.56 us: gather_features(): right = jnp.dot(hidden[1], weight, preferred_element_type=f32)]
    all_gather x2, waiting for transfers between devices: 30.8 us -> 49.3 us  [the longest x1 41.9 us: gather_features(): whole = lax.all_gather(mine, ('crop', 'dp'), axis=0, tiled=True)]
    reduce_scatter x1 -> x0, local copies, waits for them, and re-layouts: 9.12 us -> none  [body(): lax.psum_scatter(left_part + right_part, 'crop', scatter_dimension=0, til...]
    all_to_all x0 -> x2, local copies, waits for them, and re-layouts: none -> 7.2 us  [body(): lax.all_to_all(hidden, 'crop', split_axis=2, concat_axis=1, tiled=True)]
    another operation x1 -> x2, local copies, waits for them, and re-layouts: 0.04 us -> 6.39 us  [the longest x1 3.77 us: body(): hidden = jnp.stack([hidden_a, hidden_b])]
  transfers between devices with their start and end apart: 4 -> 4, of which waited for: 4 -> 3; matrix products, arithmetic and copies ran while one was open for 0% -> 14% of each run, Pallas kernels for 0% -> 0%
where the time goes in v1:
time: 184 us; the launch traced here: 183 us
  waiting for transfers between devices  84.1 us (46%)
  matrix products  26.4 us (14%)
  blocking collectives  25.3 us (14%)
  local copies, waits for them, and re-layouts  16.2 us (9%)
  other arithmetic  13.6 us (7%)
  between operations  13.2 us (7%)
  starting transfers between devices  4.59 us (2%)
    all_gather x1, waiting for transfers between devices, gather_features(): whole = lax.all_gather(mine, ('crop', 'dp'), axis=0, tiled=True)  41.9 us
    reduce_scatter x1, waiting for transfers between devices, gather_features(): lax.psum_scatter(jnp.stack([left, right], axis=1), 'dp', scatter_dimensio...  34.7 us
    psum x1, blocking collectives, share_gram(): gram = lax.psum(gram, 'tensor').astype(bf16)  25.3 us
    dot_general x1, matrix products, gather_features(): right = jnp.dot(hidden[1], weight, preferred_element_type=f32)  8.56 us
    all_gather x1, waiting for transfers between devices, share_gram(): return lax.all_gather(gram, ('crop', 'dp'), axis=1, tiled=True)  7.44 us
    all_to_all x2, local copies, waits for them, and re-layouts, body(): lax.all_to_all(hidden, 'crop', split_axis=2, concat_axis=1, tiled=True)  7.2 us
    dot_general x1, matrix products, body(): jnp.einsum('vrb,vbf->vrf', gram_low, rounded, preferred_element_type=f32)  7.19 us
    dot_general x1, matrix products, body(): return lax.dot_general(both, grads, across, preferred_element_type=f32)  6.8 us
  transfers between devices with their start and end apart: 4, of which 3 were waited for; matrix products, arithmetic and copies ran while one was open for 14% of the time, Pallas kernels for 0%

profile of v1, /device:TPU:0, one launch (start us, length us, event | category | flops | bytes accessed | tf_op | source)
XLA Modules:
  0.0 183.4 jit_solution(6360008670514362610)
XLA Ops:
  6.5 8.6 %convolution_bitcast_fusion = f32[128,1,2048]{2,0,1:T(8,128)S(1)} fusion(bf16[128,4096]{1,0:T(8,128)(2,1)} %param.4, bf16[4096,2048]{1,0:T(8,128)(2,1)} %param.5), kind=kOutput, calls=%fused_computation.9 | convolution fusion | flops 2147483648 | bytes 18874368 | tf_op jit(solution)/shard_map/dot_general | solution.py:13
  15.1 2.6 %copy-done = bf16[4096,2048]{1,0:T(8,128)(2,1)S(1)} copy-done((bf16[4096,2048]{1,0:T(8,128)(2,1)S(1)}, bf16[4096,2048]{1,0:T(8,128)(2,1)}, u32[]{:S(2)}) %copy-start) | copy-done | bytes 16777240
  17.7 2.4 %convolution_bitcast_fusion.1 = f32[128,1,2048]{2,0,1:T(8,128)S(1)} fusion(bf16[128,4096]{1,0:T(8,128)(2,1)S(1)} %copy-done.3, bf16[4096,2048]{1,0:T(8,128)(2,1)S(1)} %copy-done), kind=kOutput, calls=%fused_computation.10 | convolution fusion | flops 2147483648 | bytes 18874368 | tf_op jit(solution)/shard_map/dot_general | solution.py:12
  20.2 1.5 pad_maximum_fusion.2
  21.7 0.0 all-gather.3.cloned.1.call-start
  21.7 34.7 %reduce-scatter.2.cloned.1.call-done = f32[64,2,2048]{2,0,1:T(8,128)} async-done(((f32[128,2,2048]{2,0,1:T(8,128)}), f32[64,2,2048]{2,0,1:T(8,128)}) %reduce-scatter.2.cloned.1.call-update) | async-done | bytes 1048592 | tf_op jit(solution)/shard_map/reduce_scatter | solution.py:14
  56.4 2.1 %convert_element_type.15 = bf16[64,2,2048]{2,0,1:T(8,128)(2,1)} convert(f32[64,2,2048]{2,0,1:T(8,128)} %reduce-scatter.2.cloned.1.call-done) | non-fusion elementwise | flops 262144 | bytes 1572864 | tf_op jit(solution)/shard_map/convert_element_type | solution.py:16
  58.6 1.4 pad_maximum_fusion.1
  60.0 3.8 %copy.11 = bf16[2,128,4096]{1,0,2:T(2,128)(2,1)} copy(bf16[2,128,4096]{2,1,0:T(8,128)(2,1)S(1)} %pad_maximum_fusion.1) | data formatting | bytes 4194304 | tf_op jit(solution)/shard_map/stack | solution.py:32
  63.8 4.5 %all-to-all-start = ((bf16[2,128,4096]{1,0,2:T(2,128)(2,1)}), bf16[2,128,4096]{1,0,2:T(2,128)(2,1)}, u32[]{:S(2)}, u32[]{:S(2)}) async-start(bf16[2,128,4096]{1,0,2:T(2,128)(2,1)} %copy.11), calls=%async_computation | async-start | bytes 4194304 | tf_op jit(solution)/shard_map/all_to_all | solution.py:33
  68.3 0.0 all-gather.5.cloned.1.call-start
  68.3 41.9 %all-gather.3.cloned.1.call-done = bf16[512,2,2048]{2,0,1:T(8,128)(2,1)} async-done(((bf16[64,2,2048]{2,0,1:T(8,128)(2,1)}), bf16[512,2,2048]{2,0,1:T(8,128)(2,1)}) %all-gather.3.cloned.1.call-update) | async-done | bytes 4194320 | tf_op jit(solution)/shard_map/all_gather | solution.py:17
  110.2 2.6 %slice_bitcast_fusion.1 = (bf16[1,512,2048]{2,1,0:T(8,128)(2,1)S(1)}, bf16[1,512,2048]{2,1,0:T(8,128)(2,1)S(1)}) fusion(bf16[512,2,2048]{2,0,1:T(8,128)(2,1)} %all-gather.3.cloned.1.call-done), kind=kLoop, calls=%fused_computation.12 | loop fusion | bytes 8388608 | tf_op jit(solution)/shard_map/stack;squeeze | solution.py:18
  112.8 0.8 convert_reduce_fusion
  113.6 1.4 subtract_convert_fusion
  115.0 1.4 fusion.3
  116.4 25.3 %all-reduce.1 = bf16[2,64,512]{2,1,0:T(8,128)(2,1)} all-reduce(f32[2,64,512]{2,1,0:T(8,128)S(1)} %fusion.3), channel_id=1, replica_groups=mesh['dp'=2,'crop'=4,'tensor'=4] {'tensor'}, use_global_device_ids=true, to_apply=%region_3.0 | all-reduce | flops 65536 | bytes 393216 | tf_op jit(solution)/shard_map/psum | solution.py:27
  141.7 3.2 %copy.12 = bf16[2,128,4096]{1,2,0:T(8,128)(2,1)} copy(bf16[2,128,4096]{1,0,2:T(2,128)(2,1)} %all-to-all-done) | data formatting | bytes 4194304 | tf_op jit(solution)/shard_map/all_to_all | solution.py:33
  144.9 4.0 %copy.13 = bf16[2,4,128,1024]{3,2,1,0:T(8,128)(2,1)} copy(bf16[2,4,128,1024]{2,3,1,0:T(8,128)(2,1)} %bitcast.23) | data formatting | bytes 4194304 | tf_op jit(solution)/shard_map/all_to_all | solution.py:33
  148.9 2.1 %fusion.6 = f32[2,512,2048]{2,1,0:T(8,128)S(1)} fusion(bf16[1,512,2048]{2,1,0:T(8,128)(2,1)} %copy-done.1, bf16[1,512,2048]{2,1,0:T(8,128)(2,1)S(1)} %get-tuple-element.9), kind=kLoop, calls=%fused_computation.20 | loop fusion | flops 4194304 | bytes 12582912 | tf_op jit(solution)/shard_map/convert_element_type | solution.py:35
  151.1 4.3 %fusion.7 = (f32[1,512,2048]{2,1,0:T(8,128)}, f32[1,512,2048]{2,1,0:T(8,128)}) fusion(f32[2,512,2048]{2,1,0:T(8,128)S(1)} %fusion.6), kind=kLoop, calls=%fused_computation.21 | loop fusion | flops 2097152 | bytes 16777216 | tf_op jit(solution)/shard_map/neg | solution.py:48
  155.4 7.4 %all-gather.5.cloned.1.call-done = bf16[2,512,512]{2,1,0:T(8,128)(2,1)} async-done(((bf16[2,64,512]{2,1,0:T(8,128)(2,1)}), bf16[2,512,512]{2,1,0:T(8,128)(2,1)}) %all-gather.5.cloned.1.call-update) | async-done | bytes 1048592 | tf_op jit(solution)/shard_map/all_gather | solution.py:28
  162.8 7.2 %fusion.2 = bf16[2,512,2048]{2,1,0:T(8,128)(2,1)S(1)} fusion(f32[1,512,2048]{2,1,0:T(8,128)} %get-tuple-element.5, f32[1,512,2048]{2,1,0:T(8,128)} %get-tuple-element.6, f32[2,2048]{1,0:T(2,128)S(1)} %get-tuple-element.8, f32[2,2048]{1,0:T(2,128)S(1)} %compare_select_fusion, f32[2,2048]{1,0:T(2,128)S(1)} %broadcast_multiply_fusion, ...), kind=kOutput, calls=%fused_computation.3 | convolution fusion | flops 2181038080 | bytes 17874944 | tf_op jit(solution)/shard_map/vrb,vbf->vrf/dot_general | solution.py:43
  170.1 6.8 %fusion.8 = f32[1024,2048]{1,0:T(8,128)} fusion(bf16[1024,1024]{1,0:T(8,128)(2,1)S(1)} %bitcast.26, bf16[1024,2048]{1,0:T(8,128)(2,1)S(1)} %bitcast.27), kind=kOutput, calls=%fused_computation.22 | convolution fusion | flops 4294967296 | bytes 14680064 | tf_op jit(solution)/shard_map/dot_general | solution.py:56
  (16 shorter events, 0.1 us)
Async XLA Ops:
  6.5 8.6 %copy-start.3 = (bf16[128,4096]{1,0:T(8,128)(2,1)S(1)}, bf16[128,4096]{1,0:T(8,128)(2,1)}, u32[]{:S(2)}) copy-start(bf16[128,4096]{1,0:T(8,128)(2,1)} %param.3) | copy-start | bytes 3145732
  6.5 49.9 %reduce-scatter.2.cloned.1.call-start = ((), (), s32[]{:S(2)}) async-start(), calls=%async_computation.2 | async-start | bytes 3145728 | tf_op jit(solution)/shard_map/reduce_scatter | solution.py:14
  6.5 11.2 %copy-start = (bf16[4096,2048]{1,0:T(8,128)(2,1)S(1)}, bf16[4096,2048]{1,0:T(8,128)(2,1)}, u32[]{:S(2)}) copy-start(bf16[4096,2048]{1,0:T(8,128)(2,1)} %param.5) | copy-start | bytes 50331652
  20.2 38.4 %copy-start.2 = (bf16[128,4096]{1,0:T(8,128)(2,1)S(1)}, bf16[128,4096]{1,0:T(8,128)(2,1)}, u32[]{:S(2)}) copy-start(bf16[128,4096]{1,0:T(8,128)(2,1)} %param.4) | copy-start | bytes 3145732
  21.7 88.5 %all-gather.3.cloned.1.call-start = ((), (), s32[]{:S(2)}) async-start(), calls=%async_computation.3 | async-start | bytes 4718592 | tf_op jit(solution)/shard_map/all_gather | solution.py:17
  63.8 78.0 %all-to-all-start = ((bf16[2,128,4096]{1,0,2:T(2,128)(2,1)}), bf16[2,128,4096]{1,0,2:T(2,128)(2,1)}, u32[]{:S(2)}, u32[]{:S(2)}) async-start(bf16[2,128,4096]{1,0,2:T(2,128)(2,1)} %copy.11), calls=%async_computation | async-start | bytes 4194304 | tf_op jit(solution)/shard_map/all_to_all | solution.py:33
  68.3 94.6 %all-gather.5.cloned.1.call-start = ((), (), s32[]{:S(2)}) async-start(), calls=%async_computation.4 | async-start | bytes 1179648 | tf_op jit(solution)/shard_map/all_gather | solution.py:28
  112.8 2.2 %copy-start.1 = (bf16[1,512,2048]{2,1,0:T(8,128)(2,1)}, bf16[1,512,2048]{2,1,0:T(8,128)(2,1)S(1)}, u32[]{:S(2)}) copy-start(bf16[1,512,2048]{2,1,0:T(8,128)(2,1)S(1)} %get-tuple-element.10) | copy-start | bytes 6291460
  162.8 7.2 %copy-start.4 = (bf16[2,4,128,1024]{3,2,1,0:T(8,128)(2,1)S(1)}, bf16[2,4,128,1024]{3,2,1,0:T(8,128)(2,1)}, u32[]{:S(2)}) copy-start(bf16[2,4,128,1024]{3,2,1,0:T(8,128)(2,1)} %copy.13) | copy-start | bytes 6291460
Sparse Core Ops, SparseCore 0:
  21.8 34.6 reduce-scatter.1
  58.7 51.4 all-gather.2
  141.9 20.9 all-gather.4

commit v2 on v1

--- a/solution.py
+++ b/solution.py
@@ -8,30 +8,40 @@
 bf16 = jnp.bfloat16
 
 
-def gather_features(hidden, weight):
-    left = jnp.dot(hidden[0], weight, preferred_element_type=f32)
-    right = jnp.dot(hidden[1], weight, preferred_element_type=f32)
-    mine = lax.psum_scatter(
-        jnp.stack([left, right], axis=1), "dp", scatter_dimension=0, tiled=True
-    ).astype(bf16)
-    whole = lax.all_gather(mine, ("crop", "dp"), axis=0, tiled=True)
-    return jnp.stack([whole[:, 0, :], whole[:, 1, :]])
+def project(hidden, weight):
+    both = jnp.concatenate(hidden, axis=0)
+    part = jnp.dot(both, weight, preferred_element_type=f32)
+    return lax.psum_scatter(part, "dp", scatter_dimension=0, tiled=True).astype(bf16)
+
+
+def gather_features(mine, view_rows):
+    rows, features = mine.shape
+    crops = lax.axis_size("crop")
+    pieces = view_rows // rows
+    whole = lax.all_gather(mine, ("dp", "crop"), axis=0, tiled=True)
+    ordered = whole.reshape(2, pieces, crops, rows, features).transpose(0, 2, 1, 3, 4)
+    return ordered.reshape(2, crops * view_rows, features)
 
 
 def share_gram(rounded):
-    groups = lax.axis_size("dp") * lax.axis_size("crop")
-    rows = rounded.shape[1] // groups
-    place = lax.axis_index("crop") * lax.axis_size("dp") + lax.axis_index("dp")
-    own = lax.dynamic_slice_in_dim(rounded, place * rows, rows, axis=1)
-    gram = jnp.einsum("vrf,vbf->vrb", own, rounded, preferred_element_type=f32)
+    _, total, features = rounded.shape
+    crops = lax.axis_size("crop")
+    groups = lax.axis_size("dp") * crops
+    rows = 2 * total // groups
+    place = lax.axis_index("dp") * crops + lax.axis_index("crop")
+    own = lax.dynamic_slice_in_dim(rounded.reshape(2 * total, features), place * rows, rows)
+    view = lax.dynamic_index_in_dim(rounded, place * rows // total, keepdims=False)
+    gram = lax.dot_general(own, view, (((1,), (1,)), ((), ())), preferred_element_type=f32)
     gram = lax.psum(gram, "tensor").astype(bf16)
-    return lax.all_gather(gram, ("crop", "dp"), axis=1, tiled=True)
+    return lax.all_gather(gram, ("dp", "crop"), axis=0, tiled=True).reshape(2, total, total)
 
 
 def body(hidden_a, hidden_b, weight):
     hidden = jnp.stack([hidden_a, hidden_b])
     columns = lax.all_to_all(hidden, "crop", split_axis=2, concat_axis=1, tiled=True)
-    low = gather_features((hidden_a, hidden_b), weight)
+    mine = project((hidden_a, hidden_b), weight)
+    mine, columns = lax.optimization_barrier((mine, columns))
+    low = gather_features(mine, hidden_a.shape[0])
     stacked = low.astype(f32)
     total_rows = stacked.shape[1]
     col_means = jnp.mean(stacked, axis=1)

time: 184 us -> 175 us (0.951)
  waiting for transfers between devices: 84.1 us -> 49.6 us
  blocking collectives: 25.3 us -> 55 us
  starting transfers between devices: 4.59 us -> 0.09 us
  other arithmetic: 13.6 us -> 17.9 us
  local copies, waits for them, and re-layouts: 16.2 us -> 12 us
    reduce_scatter x1, waiting for transfers between devices: 34.7 us -> 0.01 us  [project(): lax.psum_scatter(part, 'dp', scatter_dimension=0, tiled=True).astype(bf16)]
    all_to_all x0 -> x1, blocking collectives: none -> 29.7 us  [body(): lax.all_to_all(hidden, 'crop', split_axis=2, concat_axis=1, tiled=True)]
    dot_general x1, matrix products: 6.8 us -> 13.9 us  [body(): return lax.dot_general(both, grads, across, preferred_element_type=f32)]
    dot_general x4 -> x2, matrix products: 19.6 us -> 13.2 us  [the longest x1 12.4 us: project(): part = jnp.dot(both, weight, preferred_element_type=f32)]
    all_to_all x1 -> x0, starting transfers between devices: 4.51 us -> none  [body(): lax.all_to_all(hidden, 'crop', split_axis=2, concat_axis=1, tiled=True)]
    neg x1, other arithmetic: 4.28 us -> 8.46 us  [body(): pull_term = jnp.stack([differ, -differ]) * (50.0 / total_rows)]
    all_to_all x2, local copies, waits for them, and re-layouts: 7.2 us -> 3.85 us  [body(): lax.all_to_all(hidden, 'crop', split_axis=2, concat_axis=1, tiled=True)]
    another operation x1 -> x0, local copies, waits for them, and re-layouts: 2.62 us -> none  [gather_features(): return jnp.stack([whole[:, 0, :], whole[:, 1, :]])]
  transfers between devices with their start and end apart: 4 -> 3, of which waited for: 3 -> 2; matrix products, arithmetic and copies ran while one was open for 14% -> 9% of each run, Pallas kernels for 0% -> 0%
where the time goes in v2:
time: 175 us
  blocking collectives  55 us (31%)
  waiting for transfers between devices  49.6 us (28%)
  matrix products  27.1 us (15%)
  other arithmetic  17.9 us (10%)
  between operations  13.2 us (8%)
  local copies, waits for them, and re-layouts  12 us (7%)
    all_gather x1, waiting for transfers between devices, gather_features(): whole = lax.all_gather(mine, ('dp', 'crop'), axis=0, tiled=True)  37 us
    all_to_all x1, blocking collectives, body(): lax.all_to_all(hidden, 'crop', split_axis=2, concat_axis=1, tiled=True)  29.7 us
    psum x1, blocking collectives, share_gram(): gram = lax.psum(gram, 'tensor').astype(bf16)  25.3 us
    dot_general x1, matrix products, body(): return lax.dot_general(both, grads, across, preferred_element_type=f32)  13.9 us
    all_gather x1, waiting for transfers between devices, share_gram(): lax.all_gather(gram, ('dp', 'crop'), axis=0, tiled=True)  12.6 us
    dot_general x1, matrix products, project(): part = jnp.dot(both, weight, preferred_element_type=f32)  12.4 us
    neg x1, other arithmetic, body(): pull_term = jnp.stack([differ, -differ]) * (50.0 / total_rows)  8.46 us
    another operation x1, local copies, waits for them, and re-layouts, body(): hidden = jnp.stack([hidden_a, hidden_b])  4.72 us
  transfers between devices with their start and end apart: 3, of which 2 were waited for; matrix products, arithmetic and copies ran while one was open for 9% of the time, Pallas kernels for 0%

profile of v2, /device:TPU:0, one launch (start us, length us, event | category | flops | bytes accessed | tf_op | source)
XLA Modules:
  0.0 175.0 jit_solution(973060263210842696)
XLA Ops:
  6.5 12.4 %fusion.12 = f32[256,2048]{1,0:T(8,128)} fusion(bf16[4096,2048]{1,0:T(8,128)(2,1)} %param.5, bf16[128,4096]{1,0:T(8,128)(2,1)} %param.4, bf16[128,4096]{1,0:T(8,128)(2,1)} %param.3), kind=kOutput, calls=%fused_computation.16 | convolution fusion | flops 4299161600 | bytes 20971520 | tf_op jit(solution)/shard_map/dot_general | solution.py:13
  18.9 0.0 reduce-scatter.2.cloned.1.call-update
  18.9 0.0 all-gather.3.cloned.1.call-start
  19.0 1.5 pad_maximum_fusion
  20.5 4.7 %copy.8 = bf16[2,128,4096]{1,0,2:T(2,128)(2,1)S(1)} copy(bf16[2,128,4096]{2,1,0:T(8,128)(2,1)} %pad_maximum_fusion) | data formatting | bytes 4194304 | tf_op jit(solution)/shard_map/stack | solution.py:40
  25.2 29.7 %all_to_all.18 = bf16[2,128,4096]{1,0,2:T(2,128)(2,1)S(1)} all-to-all(bf16[2,128,4096]{1,0,2:T(2,128)(2,1)S(1)} %copy.8), channel_id=1, replica_groups=mesh['dp'=2,'crop'=4,'tensor'=4] {'crop'}, dimensions={2} | all-to-all | bytes 4194304 | tf_op jit(solution)/shard_map/all_to_all | solution.py:41
  55.0 1.6 copy.9
  56.6 2.2 %all_to_all.16 = bf16[2,512,1024]{1,2,0:T(8,128)(2,1)} reshape(bf16[2,4,128,1024]{2,1,3,0:T(4,128)(2,1)S(1)} %copy.9) | data formatting | bytes 4194304 | tf_op jit(solution)/shard_map/all_to_all | solution.py:41
  58.8 2.1 %convert_element_type.22 = bf16[128,2048]{1,0:T(8,128)(2,1)} convert(f32[128,2048]{1,0:T(8,128)} %reduce-scatter.2.cloned.1.call-done) | non-fusion elementwise | flops 262144 | bytes 1572864 | tf_op jit(solution)/shard_map/convert_element_type | solution.py:14
  60.9 0.0 all-gather.3.cloned.1.call-update
  60.9 0.0 all-gather.5.cloned.1.call-start
  61.0 37.0 %all-gather.3.cloned.1.call-done = bf16[1024,2048]{1,0:T(8,128)(2,1)} async-done(((bf16[128,2048]{1,0:T(8,128)(2,1)}), bf16[1024,2048]{1,0:T(8,128)(2,1)}) %all-gather.3.cloned.1.call-update) | async-done | bytes 4194320 | tf_op jit(solution)/shard_map/all_gather | solution.py:21
  98.0 3.1 %bitcast_reduce_fusion = f32[2,2048]{1,0:T(2,128)S(1)} fusion(bf16[1024,2048]{1,0:T(8,128)(2,1)} %all-gather.3.cloned.1.call-done), kind=kLoop, calls=%fused_computation.5 | loop fusion | flops 4190208 | bytes 4210688 | tf_op jit(solution)/shard_map/reduce_sum | solution.py:47
  101.1 0.3 copy-done.1
  101.4 1.1 convert_element_type.23
  102.5 1.6 fusion.3
  104.1 1.0 sub.33
  105.2 0.8 copy-done
  106.0 1.2 copy-done.2
  107.2 0.9 fusion.16
  108.1 25.3 %all-reduce.1 = bf16[128,512]{1,0:T(8,128)(2,1)} all-reduce(f32[128,512]{1,0:T(8,128)S(1)} %fusion.16), channel_id=1, replica_groups=mesh['dp'=2,'crop'=4,'tensor'=4] {'tensor'}, use_global_device_ids=true, to_apply=%region_3.4 | all-reduce | flops 65536 | bytes 393216 | tf_op jit(solution)/shard_map/psum | solution.py:35
  133.5 8.5 %fusion.26 = (f32[1,512,2048]{2,1,0:T(8,128)}, f32[1,512,2048]{2,1,0:T(8,128)}) fusion(f32[1024,2048]{1,0:T(8,128)} %copy-done), kind=kLoop, calls=%fused_computation.33 | loop fusion | flops 2097152 | bytes 16777216 | tf_op jit(solution)/shard_map/neg | solution.py:58
  141.9 12.6 %all-gather.5.cloned.1.call-done = bf16[1024,512]{1,0:T(8,128)(2,1)} async-done(((bf16[128,512]{1,0:T(8,128)(2,1)}), bf16[1024,512]{1,0:T(8,128)(2,1)}) %all-gather.5.cloned.1.call-update) | async-done | bytes 1048592 | tf_op jit(solution)/shard_map/all_gather | solution.py:36
  154.5 13.9 %convolution_bitcast_fusion = f32[1024,2048]{1,0:T(8,128)} fusion(bf16[2,512,1024]{1,2,0:T(8,128)(2,1)S(1)} %copy-done.3, f32[1,512,2048]{2,1,0:T(8,128)} %get-tuple-element.9, f32[1,512,2048]{2,1,0:T(8,128)} %get-tuple-element.10, bf16[1024,2048]{1,0:T(8,128)(2,1)} %all-gather.3.cloned.1.call-done, f32[2,2048]{1,0:T(2,128)S(1)} %get-tuple-element.12, ...), kind=kOutput, calls=%fused_computation.8 | convolution fusion | flops 6465519616 | bytes 28360704 | tf_op jit(solution)/shard_map/dot_general | solution.py:66
  (14 shorter events, 0.1 us)
Async XLA Ops:
  6.5 12.5 %copy-start.4 = (bf16[128,4096]{1,0:T(8,128)(2,1)S(1)}, bf16[128,4096]{1,0:T(8,128)(2,1)}, u32[]{:S(2)}) copy-start(bf16[128,4096]{1,0:T(8,128)(2,1)} %param.4) | copy-start | bytes 3145732
  6.5 12.5 %copy-start.5 = (bf16[128,4096]{1,0:T(8,128)(2,1)S(1)}, bf16[128,4096]{1,0:T(8,128)(2,1)}, u32[]{:S(2)}) copy-start(bf16[128,4096]{1,0:T(8,128)(2,1)} %param.3) | copy-start | bytes 3145732
  6.5 52.3 %reduce-scatter.2.cloned.1.call-start = ((), (), s32[]{:S(2)}) async-start(), calls=%async_computation.2 | async-start | bytes 3145728 | tf_op jit(solution)/shard_map/reduce_scatter | solution.py:14
  18.9 79.0 %all-gather.3.cloned.1.call-start = ((), (), s32[]{:S(2)}) async-start(), calls=%async_computation.3 | async-start | bytes 4718592 | tf_op jit(solution)/shard_map/all_gather | solution.py:21
  60.9 93.6 %all-gather.5.cloned.1.call-start = ((), (), s32[]{:S(2)}) async-start(), calls=%async_computation.4 | async-start | bytes 1179648 | tf_op jit(solution)/shard_map/all_gather | solution.py:36
  98.0 3.4 %copy-start.1 = (bf16[1024,2048]{1,0:T(8,128)(2,1)S(1)}, bf16[1024,2048]{1,0:T(8,128)(2,1)}, u32[]{:S(2)}) copy-start(bf16[1024,2048]{1,0:T(8,128)(2,1)} %all-gather.3.cloned.1.call-done) | copy-start | bytes 12582916
  102.5 3.5 %copy-start = (f32[1024,2048]{1,0:T(8,128)}, f32[1024,2048]{1,0:T(8,128)S(1)}, u32[]{:S(2)}) copy-start(f32[1024,2048]{1,0:T(8,128)S(1)} %convert_element_type.23) | copy-start | bytes 25165828
  104.1 3.1 %copy-start.2 = (bf16[2,512,2048]{2,1,0:T(8,128)(2,1)}, bf16[2,512,2048]{2,1,0:T(8,128)(2,1)S(1)}, u32[]{:S(2)}) copy-start(bf16[2,512,2048]{2,1,0:T(8,128)(2,1)S(1)} %get-tuple-element.11) | copy-start | bytes 12582916
  133.5 21.1 %copy-start.3 = (bf16[2,512,1024]{1,2,0:T(8,128)(2,1)S(1)}, bf16[2,512,1024]{1,2,0:T(8,128)(2,1)}, u32[]{:S(2)}) copy-start(bf16[2,512,1024]{1,2,0:T(8,128)(2,1)} %all_to_all.16) | copy-start | bytes 6291460
Sparse Core Ops, SparseCore 0:
  19.1 34.6 reduce-scatter.1
  61.1 36.8 all-gather.2
  133.5 20.9 all-gather.4

commit v3 on v2

--- a/solution.py
+++ b/solution.py
@@ -32,8 +32,11 @@
     own = lax.dynamic_slice_in_dim(rounded.reshape(2 * total, features), place * rows, rows)
     view = lax.dynamic_index_in_dim(rounded, place * rows // total, keepdims=False)
     gram = lax.dot_general(own, view, (((1,), (1,)), ((), ())), preferred_element_type=f32)
-    gram = lax.psum(gram, "tensor").astype(bf16)
-    return lax.all_gather(gram, ("dp", "crop"), axis=0, tiled=True).reshape(2, total, total)
+    shares = lax.axis_size("tensor")
+    slabs = lax.all_to_all(gram, "tensor", split_axis=0, concat_axis=0, tiled=True)
+    summed = jnp.sum(slabs.reshape(shares, rows // shares, total), axis=0).astype(bf16)
+    whole = lax.all_gather(summed, ("dp", "crop", "tensor"), axis=0, tiled=True)
+    return whole.reshape(2, total, total)
 
 
 def body(hidden_a, hidden_b, weight):

time: 175 us -> 198 us (1.13)
  waiting for transfers between devices: 49.6 us -> 80.5 us
  blocking collectives: 55 us -> 43.4 us
  local copies, waits for them, and re-layouts: 12 us -> 14.2 us
    all_gather x1, waiting for transfers between devices: 12.6 us -> 43.5 us  [share_gram(): whole = lax.all_gather(summed, ('dp', 'crop', 'tensor'), axis=0, tiled=True)]
    psum x1 -> x0, blocking collectives: 25.3 us -> none  [share_gram(): gram = lax.psum(gram, 'tensor').astype(bf16)]
    all_to_all x0 -> x1, blocking collectives: none -> 13.7 us  [share_gram(): lax.all_to_all(gram, 'tensor', split_axis=0, concat_axis=0, tiled=True)]
    unnamed x12, local copies, waits for them, and re-layouts: 2.38 us -> 4.64 us
  transfers between devices with their start and end apart: 3 -> 3, of which waited for: 2 -> 2; matrix products, arithmetic and copies ran while one was open for 9% -> 8% of each run, Pallas kernels for 0% -> 0%
where the time goes in v3:
time: 198 us; the launch traced here: 197 us
  waiting for transfers between devices  80.5 us (41%)
  blocking collectives  43.4 us (22%)
  matrix products  27.1 us (14%)
  other arithmetic  18.7 us (9%)
  local copies, waits for them, and re-layouts  14.2 us (7%)
  between operations  13.2 us (7%)
    all_gather x1, waiting for transfers between devices, share_gram(): whole = lax.all_gather(summed, ('dp', 'crop', 'tensor'), axis=0, tiled=True)  43.5 us
    all_gather x1, waiting for transfers between devices, gather_features(): whole = lax.all_gather(mine, ('dp', 'crop'), axis=0, tiled=True)  37 us
    all_to_all x1, blocking collectives, body(): lax.all_to_all(hidden, 'crop', split_axis=2, concat_axis=1, tiled=True)  29.7 us
    dot_general x1, matrix products, body(): return lax.dot_general(both, grads, across, preferred_element_type=f32)  13.9 us
    all_to_all x1, blocking collectives, share_gram(): lax.all_to_all(gram, 'tensor', split_axis=0, concat_axis=0, tiled=True)  13.7 us
    dot_general x1, matrix products, project(): part = jnp.dot(both, weight, preferred_element_type=f32)  12.4 us
    neg x1, other arithmetic, body(): pull_term = jnp.stack([differ, -differ]) * (50.0 / total_rows)  8.5 us
    another operation x1, local copies, waits for them, and re-layouts, body(): hidden = jnp.stack([hidden_a, hidden_b])  4.72 us
  transfers between devices with their start and end apart: 3, of which 2 were waited for; matrix products, arithmetic and copies ran while one was open for 8% of the time, Pallas kernels for 0%

profile of v3, /device:TPU:0, one launch (start us, length us, event | category | flops | bytes accessed | tf_op | source)
XLA Modules:
  0.0 197.3 jit_solution(16633008843241418453)
XLA Ops:
  6.5 12.4 %fusion.12 = f32[256,2048]{1,0:T(8,128)} fusion(bf16[4096,2048]{1,0:T(8,128)(2,1)} %param.5, bf16[128,4096]{1,0:T(8,128)(2,1)} %param.4, bf16[128,4096]{1,0:T(8,128)(2,1)} %param.3), kind=kOutput, calls=%fused_computation.16 | convolution fusion | flops 4299161600 | bytes 20971520 | tf_op jit(solution)/shard_map/dot_general | solution.py:13
  18.9 0.0 all-gather.3.cloned.1.call-start
  19.0 1.5 pad_maximum_fusion
  20.5 4.7 %copy.8 = bf16[2,128,4096]{1,0,2:T(2,128)(2,1)S(1)} copy(bf16[2,128,4096]{2,1,0:T(8,128)(2,1)} %pad_maximum_fusion) | data formatting | bytes 4194304 | tf_op jit(solution)/shard_map/stack | solution.py:43
  25.2 29.7 %all_to_all.24 = bf16[2,128,4096]{1,0,2:T(2,128)(2,1)S(1)} all-to-all(bf16[2,128,4096]{1,0,2:T(2,128)(2,1)S(1)} %copy.8), channel_id=1, replica_groups=mesh['dp'=2,'crop'=4,'tensor'=4] {'crop'}, dimensions={2} | all-to-all | bytes 4194304 | tf_op jit(solution)/shard_map/all_to_all | solution.py:44
  55.0 1.6 copy.9
  56.6 2.2 %all_to_all.20 = bf16[2,512,1024]{1,2,0:T(8,128)(2,1)} reshape(bf16[2,4,128,1024]{2,1,3,0:T(4,128)(2,1)S(1)} %copy.9) | data formatting | bytes 4194304 | tf_op jit(solution)/shard_map/all_to_all | solution.py:44
  58.8 2.1 %convert_element_type.22 = bf16[128,2048]{1,0:T(8,128)(2,1)} convert(f32[128,2048]{1,0:T(8,128)} %reduce-scatter.2.cloned.1.call-done) | non-fusion elementwise | flops 262144 | bytes 1572864 | tf_op jit(solution)/shard_map/convert_element_type | solution.py:14
  60.9 0.0 all-gather.5.cloned.1.call-start
  61.0 37.0 %all-gather.3.cloned.1.call-done = bf16[1024,2048]{1,0:T(8,128)(2,1)} async-done(((bf16[128,2048]{1,0:T(8,128)(2,1)}), bf16[1024,2048]{1,0:T(8,128)(2,1)}) %all-gather.3.cloned.1.call-update) | async-done | bytes 4194320 | tf_op jit(solution)/shard_map/all_gather | solution.py:21
  98.0 3.1 %bitcast_reduce_fusion = f32[2,2048]{1,0:T(2,128)S(1)} fusion(bf16[1024,2048]{1,0:T(8,128)(2,1)} %all-gather.3.cloned.1.call-done), kind=kLoop, calls=%fused_computation.5 | loop fusion | flops 4190208 | bytes 4210688 | tf_op jit(solution)/shard_map/reduce_sum | solution.py:50
  101.1 0.3 copy-done.1
  101.4 1.1 convert_element_type.23
  102.5 1.0 sub.33
  103.5 2.4 %copy-done = f32[1024,2048]{1,0:T(8,128)} copy-done((f32[1024,2048]{1,0:T(8,128)}, f32[1024,2048]{1,0:T(8,128)S(1)}, u32[]{:S(2)}) %copy-start) | copy-done | bytes 8388632
  105.9 0.2 fusion.19
  106.1 1.6 fusion.3
  107.7 2.0 copy-done.2
  109.6 0.8 fusion.16
  110.5 13.7 %all_to_all.25 = f32[4,32,512]{2,1,0:T(8,128)S(1)} all-to-all(f32[4,32,512]{2,1,0:T(8,128)S(1)} %fusion.16), channel_id=1, replica_groups=mesh['dp'=2,'crop'=4,'tensor'=4] {'tensor'}, dimensions={0} | all-to-all | bytes 524288 | tf_op jit(solution)/shard_map/all_to_all | solution.py:36
  124.2 0.6 reduce_sum.29
  124.9 8.5 %fusion.25 = (f32[1,512,2048]{2,1,0:T(8,128)}, f32[1,512,2048]{2,1,0:T(8,128)}) fusion(f32[1024,2048]{1,0:T(8,128)} %copy-done), kind=kLoop, calls=%fused_computation.33 | loop fusion | flops 2097152 | bytes 16777216 | tf_op jit(solution)/shard_map/neg | solution.py:61
  133.4 43.5 %all-gather.5.cloned.1.call-done = bf16[1024,512]{1,0:T(8,128)(2,1)} async-done(((bf16[32,512]{1,0:T(8,128)(2,1)}), bf16[1024,512]{1,0:T(8,128)(2,1)}) %all-gather.5.cloned.1.call-update) | async-done | bytes 1048592 | tf_op jit(solution)/shard_map/all_gather | solution.py:38
  176.9 13.9 %convolution_bitcast_fusion = f32[1024,2048]{1,0:T(8,128)} fusion(bf16[2,512,1024]{1,2,0:T(8,128)(2,1)S(1)} %copy-done.3, f32[1,512,2048]{2,1,0:T(8,128)} %get-tuple-element.9, f32[1,512,2048]{2,1,0:T(8,128)} %get-tuple-element.10, bf16[1024,2048]{1,0:T(8,128)(2,1)} %all-gather.3.cloned.1.call-done, f32[2,2048]{1,0:T(2,128)S(1)} %get-tuple-element.12, ...), kind=kOutput, calls=%fused_computation.8 | convolution fusion | flops 6465519616 | bytes 28360704 | tf_op jit(solution)/shard_map/dot_general | solution.py:69
  (16 shorter events, 0.1 us)
Async XLA Ops:
  6.5 12.5 %copy-start.4 = (bf16[128,4096]{1,0:T(8,128)(2,1)S(1)}, bf16[128,4096]{1,0:T(8,128)(2,1)}, u32[]{:S(2)}) copy-start(bf16[128,4096]{1,0:T(8,128)(2,1)} %param.4) | copy-start | bytes 3145732
  6.5 12.5 %copy-start.5 = (bf16[128,4096]{1,0:T(8,128)(2,1)S(1)}, bf16[128,4096]{1,0:T(8,128)(2,1)}, u32[]{:S(2)}) copy-start(bf16[128,4096]{1,0:T(8,128)(2,1)} %param.3) | copy-start | bytes 3145732
  6.5 52.3 %reduce-scatter.2.cloned.1.call-start = ((), (), s32[]{:S(2)}) async-start(), calls=%async_computation.3 | async-start | bytes 3145728 | tf_op jit(solution)/shard_map/reduce_scatter | solution.py:14
  18.9 79.0 %all-gather.3.cloned.1.call-start = ((), (), s32[]{:S(2)}) async-start(), calls=%async_computation.4 | async-start | bytes 4718592 | tf_op jit(solution)/shard_map/all_gather | solution.py:21
  60.9 115.9 %all-gather.5.cloned.1.call-start = ((), (), s32[]{:S(2)}) async-start(), calls=%async_computation.5 | async-start | bytes 1081344 | tf_op jit(solution)/shard_map/all_gather | solution.py:38
  98.0 3.4 %copy-start.1 = (bf16[1024,2048]{1,0:T(8,128)(2,1)S(1)}, bf16[1024,2048]{1,0:T(8,128)(2,1)}, u32[]{:S(2)}) copy-start(bf16[1024,2048]{1,0:T(8,128)(2,1)} %all-gather.3.cloned.1.call-done) | copy-start | bytes 12582916
  102.5 3.4 %copy-start = (f32[1024,2048]{1,0:T(8,128)}, f32[1024,2048]{1,0:T(8,128)S(1)}, u32[]{:S(2)}) copy-start(f32[1024,2048]{1,0:T(8,128)S(1)} %convert_element_type.23) | copy-start | bytes 25165828
  107.7 2.0 %copy-start.2 = (bf16[2,512,2048]{2,1,0:T(8,128)(2,1)}, bf16[2,512,2048]{2,1,0:T(8,128)(2,1)S(1)}, u32[]{:S(2)}) copy-start(bf16[2,512,2048]{2,1,0:T(8,128)(2,1)S(1)} %get-tuple-element.11) | copy-start | bytes 12582916
  124.9 52.0 %copy-start.3 = (bf16[2,512,1024]{1,2,0:T(8,128)(2,1)S(1)}, bf16[2,512,1024]{1,2,0:T(8,128)(2,1)}, u32[]{:S(2)}) copy-start(bf16[2,512,1024]{1,2,0:T(8,128)(2,1)} %all_to_all.20) | copy-start | bytes 6291460
Sparse Core Ops, SparseCore 0:
  19.1 34.6 reduce-scatter.1
  61.1 36.8 all-gather.2
  124.9 51.9 all-gather.4
